TPU v7x, 32 devices: a whole 2x2x4 slice. The times are simulated.
32 devices in a mesh: head: 4 (over z), ctx: 8 (over y, x, core).
Axes of the slice: x: 2, y: 2, z: 4, core: 2. Of those that a mesh axis runs over, the one named last changes fastest.
Arguments:
- queries: bfloat16 [8192, 4, 128], P('ctx', 'head'), may hold values from -120 to 120
- keys: bfloat16 [8192, 4, 128], P('ctx', 'head'), may hold values from -6 to 6
- values: bfloat16 [8192, 4, 128], P('ctx', 'head'), may hold values from -6 to 6
- house: bfloat16 [8192, 4, 128], P('ctx', 'head'), may hold values from -6 to 6
- rates: float32 [4, 8192], P('head', 'ctx'), may hold values from 0.0002 to 1.9, as said below
- out_weight: bfloat16 [512, 8192], P('head'), may hold values from -0.375 to 0.375
Outputs:
- attended: bfloat16 [8192, 4, 128], P('ctx', 'head')
- projected: bfloat16 [8192, 8192], P('ctx', 'head')
Inputs may be any that keep to these rules, and one draw needn't show every extreme that they name: `rates`: strictly positive and below 2, so every transition is a contraction.
All inputs are finite; a program needn't handle non-finite values.
Results may differ from a plain program's by a relative error of at most 0.015.
Values may be sent and summed in bfloat16 or wider, within the bound.
A program may use at most 64 MiB of HBM per device.

v0:
```python
import jax
import jax.numpy as jnp
from jax import lax
from jax.sharding import PartitionSpec as P

BLOCK = 128


EPSILON = 1e-06
NEGATIVE = -1e30
PRECISE = lax.Precision.HIGHEST


def from_behind(block, axis, distance):
    devices = range(lax.axis_size(axis))
    route = [(i - distance, i) for i in devices if i - distance in devices]
    return lax.ppermute(block, axis, route)


def matmul(first_matrix, second_matrix):
    return jnp.matmul(first_matrix, second_matrix, precision=PRECISE)


def block_parts(query_rows, key_rows, house_rows, decays):
    length = query_rows.shape[0]
    features = query_rows.shape[1]
    row_index = lax.broadcasted_iota(jnp.int32, (length, length), 0)
    col_index = lax.broadcasted_iota(jnp.int32, (length, length), 1)
    gram_matrix = matmul(house_rows, house_rows.T)
    zero_block = jnp.zeros_like(gram_matrix)
    lower_part = jnp.where(row_index > col_index, gram_matrix, zero_block) + jnp.diag(1.0 / decays)
    identity = jnp.eye(length, dtype=query_rows.dtype)
    inverse = jax.scipy.linalg.solve_triangular(lower_part, identity, lower=True)
    left_part = jnp.where(row_index >= col_index, matmul(query_rows, house_rows.T), zero_block)
    right_part = matmul(
        inverse, jnp.where(row_index > col_index, matmul(house_rows, key_rows.T), zero_block)
    )
    start_query = query_rows - matmul(matmul(left_part, inverse), house_rows)
    final_key = key_rows - matmul(right_part.T, house_rows)
    inside_mask = matmul(query_rows, key_rows.T) - matmul(left_part, right_part)
    inside_mask = jnp.where(row_index >= col_index, inside_mask, NEGATIVE)
    passage = jnp.eye(features, dtype=query_rows.dtype) - matmul(
        house_rows.T, matmul(inverse, house_rows)
    )
    return (start_query, final_key, inside_mask, passage)


def shard_local(start_query, final_key, inside_mask, passage):
    blocks, length, features = start_query.shape
    rows_dev = blocks * length
    col_block = lax.broadcasted_iota(jnp.int32, (length, rows_dev), 1) // length
    anchor = jnp.zeros((), jnp.int32)

    def advance(running, element):
        moved_keys, prefix = running
        number, query_rows, key_rows, inside_rows, passage_rows = element
        across = matmul(query_rows, moved_keys.T)
        scores = jnp.where(col_block < number, across, NEGATIVE)
        scores = lax.dynamic_update_slice(scores, inside_rows, (anchor, number * length))
        carried_query = matmul(query_rows, prefix)
        moved_keys = matmul(moved_keys, passage_rows.T)
        moved_keys = lax.dynamic_update_slice(moved_keys, key_rows, (number * length, anchor))
        prefix = matmul(passage_rows, prefix)
        return ((moved_keys, prefix), (scores, carried_query))

    numbers = jnp.arange(blocks, dtype=jnp.int32)
    initial = (
        jnp.zeros((rows_dev, features), start_query.dtype),
        jnp.eye(features, dtype=start_query.dtype),
    )
    (end_keys, transit), (scores, carried) = lax.scan(
        advance, initial, (numbers, start_query, final_key, inside_mask, passage)
    )
    return (
        scores.reshape(rows_dev, rows_dev),
        carried.reshape(rows_dev, features),
        end_keys,
        transit,
    )


def transfer_table(all_ends, number):
    features = all_ends.shape[1]

    def gradient_pass(running, element):
        source, passage = element
        before = source < number
        projected_result = jnp.where(before, running, jnp.zeros_like(running))
        running = jnp.where(before, matmul(running, passage), running)
        return (running, projected_result)

    sources = jnp.arange(all_ends.shape[0], dtype=jnp.int32)
    _, transfers = lax.scan(
        gradient_pass, jnp.eye(features, dtype=all_ends.dtype), (sources, all_ends), reverse=True
    )
    return transfers


def absorb(softmax_state, query_start, transfers, key_block, value_block, source, number):
    row_peak, row_total, summed = softmax_state
    clipped = jnp.clip(source, 0, transfers.shape[0] - 1)
    passage = lax.dynamic_index_in_dim(transfers, clipped, 0, keepdims=False)
    moved_query = matmul(query_start, passage)
    scores = matmul(moved_query, key_block.astype(jnp.float32).T)
    usable = jnp.logical_and(source >= 0, source < number)
    scores = jnp.where(usable, scores, NEGATIVE)
    new_peak = jnp.maximum(row_peak, jnp.max(scores, axis=1))
    weight_matrix = jnp.where(usable, jnp.exp(scores - new_peak[:, None]), 0.0)
    shrink = jnp.exp(row_peak - new_peak)
    row_total = row_total * shrink + jnp.sum(weight_matrix, axis=1)
    summed = summed * shrink[:, None] + jnp.dot(
        weight_matrix.astype(jnp.bfloat16), value_block, preferred_element_type=jnp.float32
    )
    return (new_peak, row_total, summed)


def body(queries, keys, values, house, rates, out_weight):
    rows_dev = queries.shape[0]
    features = queries.shape[2]
    shards = lax.axis_size("ctx")
    number = lax.axis_index("ctx")
    blocks = rows_dev // BLOCK
    query_rows = queries[:, 0, :].astype(jnp.float32) * features ** (-0.5)
    key_rows = keys[:, 0, :].astype(jnp.float32)
    value_rows = values[:, 0, :]
    house_raw = house[:, 0, :].astype(jnp.float32)
    house_unit = house_raw / jnp.sqrt(
        jnp.sum(house_raw * house_raw, axis=1, keepdims=True) + EPSILON
    )
    block_data = jax.vmap(block_parts)(
        query_rows.reshape(blocks, BLOCK, features),
        key_rows.reshape(blocks, BLOCK, features),
        house_unit.reshape(blocks, BLOCK, features),
        rates[0].reshape(blocks, BLOCK),
    )
    local_scores, query_start, end_keys, transit = shard_local(*block_data)
    row_peak = jnp.max(local_scores, axis=1)
    weight_matrix = jnp.exp(local_scores - row_peak[:, None])
    row_total = jnp.sum(weight_matrix, axis=1)
    summed = jnp.dot(
        weight_matrix.astype(jnp.bfloat16), value_rows, preferred_element_type=jnp.float32
    )
    softmax_state = (row_peak, row_total, summed)
    all_ends = lax.all_gather(transit[None], "ctx", axis=0, tiled=True)
    transfers = transfer_table(all_ends, number)
    stored_keys = end_keys.astype(jnp.bfloat16)

    def travel(offset, running):
        moving, inner_state = running
        moving = from_behind((moving[0], moving[1]), "ctx", 1)
        inner_state = absorb(
            inner_state, query_start, transfers, moving[0], moving[1], number - 1 - offset, number
        )
        return (moving, inner_state)

    _, softmax_state = lax.fori_loop(
        0, shards - 1, travel, ((stored_keys, value_rows), softmax_state)
    )
    row_peak, row_total, summed = softmax_state
    attended = (summed / row_total[:, None]).astype(jnp.bfloat16)
    columns = lax.all_to_all(out_weight, "head", split_axis=1, concat_axis=0, tiled=True)
    piece = lax.all_gather(attended[:, None, :], "head", axis=1, tiled=True)
    heads_here = piece.shape[1]
    flattened = piece.reshape(piece.shape[0], heads_here * features)
    projected = jnp.dot(flattened, columns, preferred_element_type=jnp.float32)
    return (attended[:, None, :], projected.astype(jnp.bfloat16))


def solution(mesh):
    in_specs = (
        P("ctx", "head", None),
        P("ctx", "head", None),
        P("ctx", "head", None),
        P("ctx", "head", None),
        P("head", "ctx"),
        P("head", None),
    )
    out_specs = (P("ctx", "head", None), P("ctx", "head"))
    return jax.shard_map(body, mesh=mesh, in_specs=in_specs, out_specs=out_specs, check_vma=False)
```

profile of v0, /device:TPU:13, one launch (start us, length us, event | category | flops | bytes accessed | tf_op | source)
XLA Modules:
  0.0 363.8 jit_solution(12380750964197361690)
XLA Ops:
  7.2 1.7 copy.92
  8.9 3.2 copy.25
  12.1 2.7 copy.26
  14.8 4.8 %all-to-all-start = ((bf16[128,4,2048]{2,0,1:T(8,128)(2,1)}), bf16[128,4,2048]{2,0,1:T(8,128)(2,1)}, u32[]{:S(2)}, u32[]{:S(2)}) async-start(bf16[128,4,2048]{2,0,1:T(8,128)(2,1)} %copy.26), calls=%async_computation | async-start | bytes 4194304 | tf_op jit(solution)/shard_map/all_to_all | solution.py:161
  22.8 2.2 fusion.40
  25.0 79.4 %custom-call.4 = f32[8,1,128,128]{2,3,1,0:T(8,128)S(1)} custom-call(f32[8,1,128,128]{3,2,1,0:T(8,128)} %fusion.40), custom_call_target="InvertDiagBlocksLowerTriangular" | custom-call | tf_op jit(solution)/shard_map/vmap(jit(_solve_triangular))/triangular_solve | solution.py:33
  105.4 1.7 fusion.51
  108.5 2.0 convolution_subtract_fusion.2
  111.9 2.0 convolution_subtract_fusion.3
  113.9 56.5 %while.61 = (s32[]{:T(128)}, f32[1024,128]{0,1:T(8,128)S(1)}, f32[128,128]{1,0:T(8,128)S(1)}, f32[8,128,1024]{2,1,0:T(8,128)}, f32[8,128,128]{2,1,0:T(8,128)S(1)...) while((s32[]{:T(128)}, f32[1024,128]{0,1:T(8,128)S(1)}, ...), condition=%wide.region_2.3_spmd.clone.clone, body=%wide.region_1.2_spmd.clone.sunk.clone | while | flops 453378048 | bytes 5385931 | solution.py:71
  170.4 2.5 reduce_max.26
  172.8 3.0 fusion.35
  175.8 12.1 %all-gather = f32[1024,128]{1,0:T(8,128)} all-gather(f32[128,128]{1,0:T(8,128)S(1)} %get-tuple-element.404), channel_id=2, replica_groups=mesh['head'=4,'ctx'=8] {'ctx'}, dimensions={0}, use_global_device_ids=true | all-gather | bytes 589824 | tf_op jit(solution)/shard_map/all_gather | solution.py:144
  188.8 24.3 %while.59 = (s32[]{:T(128)}, f32[128,128]{0,1:T(8,128)S(1)}, f32[8,128,128]{1,2,0:T(8,128)}, s32[8]{0:T(128)S(1)}, s32[]{:T(128)}, /*index=5*/f32[8,128,128]{2,1,0:T(8,128)}) while((s32[]{:T(128)}, f32[128,128]{0,1:T(8,128)S(1)}, f32[8,128,128]{1,2,0:T(8,128)}, s32[8]{0:T(128)S(1)}, s32[]{:T(128)}, ...), condition=%wide.region_6.7_spmd.clone, body=%wide.region_5.6_spmd.sunk.clone | while | flops 25198596 | bytes 524400 | solution.py:93
  213.9 2.5 fusion.49
  216.4 99.9 %while.60 = (s32[]{:T(128)}, bf16[1024,128]{1,0:T(8,128)(2,1)}, bf16[1024,128]{1,0:T(8,128)(2,1)}, f32[1024]{0:T(1024)S(1)}, f32[1024]{0:T(1024)S(1)}, /*index=5...) while((s32[]{:T(128)}, bf16[1024,128]{1,0:T(8,128)(2,1)}, ...), condition=%wide.region_10.11_spmd.clone, body=%wide.region_7.10_spmd.sunk.clone | while | flops 2091124736 | bytes 23200044 | solution.py:156
  216.4 2.3 collective-permute-start
  218.7 2.3 collective-permute-start.1
  220.9 1.4 fusion.143
  222.4 2.0 select_reduce_fusion.3
  228.7 4.2 %collective-permute-start = (bf16[1024,128]{1,0:T(8,128)(2,1)}, bf16[1024,128]{1,0:T(8,128)(2,1)S(1)}, u32[]{:S(2)}, u32[]{:S(2)}) collective-permute-start(bf16[1024,128]{1,0:T(8,128)(2,1)} %get-tuple-element.903), channel_id=1, source_target_pairs={{0,1},{1,2},{2,3},{3,4},{4,5},{5,6},{6,7},{8,9},{9,10},{10,11},{11... | collective-permute-start | bytes 786440 | tf_op jit(solution)/shard_map/while/body/eval_jaxpr/ppermute | solution.py:17
  232.8 1.9 collective-permute-start.1
  234.8 1.4 fusion.143
  236.4 2.0 select_reduce_fusion.3
  242.7 4.3 %collective-permute-start = (bf16[1024,128]{1,0:T(8,128)(2,1)}, bf16[1024,128]{1,0:T(8,128)(2,1)S(1)}, u32[]{:S(2)}, u32[]{:S(2)}) collective-permute-start(bf16[1024,128]{1,0:T(8,128)(2,1)} %get-tuple-element.903), channel_id=1, source_target_pairs={{0,1},{1,2},{2,3},{3,4},{4,5},{5,6},{6,7},{8,9},{9,10},{10,11},{11... | collective-permute-start | bytes 786440 | tf_op jit(solution)/shard_map/while/body/eval_jaxpr/ppermute | solution.py:17
  247.0 1.9 collective-permute-start.1
  248.9 1.4 fusion.143
  250.6 2.1 select_reduce_fusion.3
  256.9 4.3 %collective-permute-start = (bf16[1024,128]{1,0:T(8,128)(2,1)}, bf16[1024,128]{1,0:T(8,128)(2,1)S(1)}, u32[]{:S(2)}, u32[]{:S(2)}) collective-permute-start(bf16[1024,128]{1,0:T(8,128)(2,1)} %get-tuple-element.903), channel_id=1, source_target_pairs={{0,1},{1,2},{2,3},{3,4},{4,5},{5,6},{6,7},{8,9},{9,10},{10,11},{11... | collective-permute-start | bytes 786440 | tf_op jit(solution)/shard_map/while/body/eval_jaxpr/ppermute | solution.py:17
  261.1 1.9 collective-permute-start.1
  263.1 1.4 fusion.143
  264.9 2.0 select_reduce_fusion.3
  271.1 4.2 %collective-permute-start = (bf16[1024,128]{1,0:T(8,128)(2,1)}, bf16[1024,128]{1,0:T(8,128)(2,1)S(1)}, u32[]{:S(2)}, u32[]{:S(2)}) collective-permute-start(bf16[1024,128]{1,0:T(8,128)(2,1)} %get-tuple-element.903), channel_id=1, source_target_pairs={{0,1},{1,2},{2,3},{3,4},{4,5},{5,6},{6,7},{8,9},{9,10},{10,11},{11... | collective-permute-start | bytes 786440 | tf_op jit(solution)/shard_map/while/body/eval_jaxpr/ppermute | solution.py:17
  275.3 1.9 collective-permute-start.1
  277.3 1.4 fusion.143
  279.9 2.0 select_reduce_fusion.3
  286.2 3.3 collective-permute-start
  289.5 1.9 collective-permute-start.1
  291.4 1.4 fusion.143
  292.9 2.1 collective-permute-done
  295.0 2.0 select_reduce_fusion.3
  301.3 2.4 collective-permute-start
  303.7 1.9 collective-permute-start.1
  305.6 1.4 fusion.143
  307.0 3.0 collective-permute-done
  310.0 2.0 select_reduce_fusion.3
  319.2 31.3 %all-gather.4.cloned.1.call-done = bf16[1024,512]{0,1:T(8,128)(2,1)} async-done(((bf16[1024,128]{0,1:T(8,128)(2,1)}), bf16[1024,512]{0,1:T(8,128)(2,1)}) %all-gather.4.cloned.1.call-update) | async-done | bytes 1048592 | tf_op jit(solution)/shard_map/all_gather | solution.py:162
  350.6 6.3 %bitcast_convert_fusion = bf16[1024,2048]{1,0:T(8,128)(2,1)} fusion(bf16[1024,4,128]{0,2,1:T(8,128)(2,1)} %bitcast.179, bf16[128,4,2048]{2,0,1:T(8,128)(2,1)} %all-to-all-done), kind=kOutput, calls=%fused_computation.45 | convolution fusion | flops 2149580800 | bytes 7340032 | tf_op jit(solution)/shard_map/dot_general | solution.py:165
  (256 shorter events, 112.2 us)
Async XLA Ops:
  12.1 7.7 %copy-start.4 = (bf16[1024,1,128]{2,0,1:T(8,128)(2,1)S(1)}, bf16[1024,1,128]{2,0,1:T(8,128)(2,1)}, u32[]{:S(2)}) copy-start(bf16[1024,1,128]{2,0,1:T(8,128)(2,1)} %param.15) | copy-start | bytes 786436
  12.1 8.0 %copy-start.8 = (f32[1,1024]{1,0:T(1,128)S(1)}, f32[1,1024]{1,0:T(1,128)}, u32[]{:S(2)}) copy-start(f32[1,1024]{1,0:T(1,128)} %param.16) | copy-start | bytes 12292
  12.1 8.0 %copy-start.2 = (bf16[1024,1,128]{2,0,1:T(8,128)(2,1)S(1)}, bf16[1024,1,128]{2,0,1:T(8,128)(2,1)}, u32[]{:S(2)}) copy-start(bf16[1024,1,128]{2,0,1:T(8,128)(2,1)} %param.12) | copy-start | bytes 786436
  12.1 8.0 %copy-start.3 = (bf16[1024,1,128]{2,0,1:T(8,128)(2,1)S(1)}, bf16[1024,1,128]{2,0,1:T(8,128)(2,1)}, u32[]{:S(2)}) copy-start(bf16[1024,1,128]{2,0,1:T(8,128)(2,1)} %param.13) | copy-start | bytes 786436
  14.8 335.7 %all-to-all-start = ((bf16[128,4,2048]{2,0,1:T(8,128)(2,1)}), bf16[128,4,2048]{2,0,1:T(8,128)(2,1)}, u32[]{:S(2)}, u32[]{:S(2)}) async-start(bf16[128,4,2048]{2,0,1:T(8,128)(2,1)} %copy.26), calls=%async_computation | async-start | bytes 4194304 | tf_op jit(solution)/shard_map/all_to_all | solution.py:161
  19.6 331.0 %all-gather.4.cloned.1.call-start = ((), (), s32[]{:S(2)}) async-start(), calls=%async_computation.1 | async-start | bytes 1310720 | tf_op jit(solution)/shard_map/all_gather | solution.py:162
  19.6 3.2 copy-start.6
  104.4 4.1 %copy-start.5 = (bf16[1024,1,128]{2,0,1:T(8,128)(2,1)S(1)}, bf16[1024,1,128]{2,0,1:T(8,128)(2,1)}, u32[]{:S(2)}) copy-start(bf16[1024,1,128]{2,0,1:T(8,128)(2,1)} %param.15) | copy-start | bytes 786436
  104.4 6.0 %copy-start.7 = (pred[128,128]{1,0:T(8,128)(4,1)S(1)}, pred[128,128]{1,0:T(8,128)(4,1)}, u32[]{:S(2)}) copy-start(pred[128,128]{1,0:T(8,128)(4,1)} %copy-done.6) | copy-start | bytes 49156
  216.4 6.0 %collective-permute-start = (bf16[1024,128]{1,0:T(8,128)(2,1)}, bf16[1024,128]{1,0:T(8,128)(2,1)S(1)}, u32[]{:S(2)}, u32[]{:S(2)}) collective-permute-start(bf16[1024,128]{1,0:T(8,128)(2,1)} %get-tuple-element.903), channel_id=1, source_target_pairs={{0,1},{1,2},{2,3},{3,4},{4,5},{5,6},{6,7},{8,9},{9,10},{10,11},{11... | collective-permute-start | bytes 786440 | tf_op jit(solution)/shard_map/while/body/eval_jaxpr/ppermute | solution.py:17
  218.7 7.4 %collective-permute-start.1 = (bf16[1024,128]{1,0:T(8,128)(2,1)}, bf16[1024,128]{1,0:T(8,128)(2,1)S(1)}, u32[]{:S(2)}, u32[]{:S(2)}) collective-permute-start(bf16[1024,128]{1,0:T(8,128)(2,1)} %get-tuple-element.904), channel_id=1, source_target_pairs={{0,1},{1,2},{2,3},{3,4},{4,5},{5,6},{6,7},{8,9},{9,10},{10,11},{11... | collective-permute-start | bytes 786440 | tf_op jit(solution)/shard_map/while/body/eval_jaxpr/ppermute | solution.py:17
  222.4 4.4 %copy-start = (f32[1024,128]{1,0:T(8,128)S(1)}, f32[1024,128]{1,0:T(8,128)}, u32[]{:S(2)}) copy-start(f32[1024,128]{1,0:T(8,128)} %get-tuple-element.907) | copy-start | bytes 1572868 | tf_op jit(solution)/shard_map/while
  227.9 0.8 copy-start.1
  228.7 7.8 %collective-permute-start = (bf16[1024,128]{1,0:T(8,128)(2,1)}, bf16[1024,128]{1,0:T(8,128)(2,1)S(1)}, u32[]{:S(2)}, u32[]{:S(2)}) collective-permute-start(bf16[1024,128]{1,0:T(8,128)(2,1)} %get-tuple-element.903), channel_id=1, source_target_pairs={{0,1},{1,2},{2,3},{3,4},{4,5},{5,6},{6,7},{8,9},{9,10},{10,11},{11... | collective-permute-start | bytes 786440 | tf_op jit(solution)/shard_map/while/body/eval_jaxpr/ppermute | solution.py:17
  232.8 7.3 %collective-permute-start.1 = (bf16[1024,128]{1,0:T(8,128)(2,1)}, bf16[1024,128]{1,0:T(8,128)(2,1)S(1)}, u32[]{:S(2)}, u32[]{:S(2)}) collective-permute-start(bf16[1024,128]{1,0:T(8,128)(2,1)} %get-tuple-element.904), channel_id=1, source_target_pairs={{0,1},{1,2},{2,3},{3,4},{4,5},{5,6},{6,7},{8,9},{9,10},{10,11},{11... | collective-permute-start | bytes 786440 | tf_op jit(solution)/shard_map/while/body/eval_jaxpr/ppermute | solution.py:17
  236.2 4.6 %copy-start = (f32[1024,128]{1,0:T(8,128)S(1)}, f32[1024,128]{1,0:T(8,128)}, u32[]{:S(2)}) copy-start(f32[1024,128]{1,0:T(8,128)} %get-tuple-element.907) | copy-start | bytes 1572868 | tf_op jit(solution)/shard_map/while
  241.9 0.8 copy-start.1
  242.7 7.9 %collective-permute-start = (bf16[1024,128]{1,0:T(8,128)(2,1)}, bf16[1024,128]{1,0:T(8,128)(2,1)S(1)}, u32[]{:S(2)}, u32[]{:S(2)}) collective-permute-start(bf16[1024,128]{1,0:T(8,128)(2,1)} %get-tuple-element.903), channel_id=1, source_target_pairs={{0,1},{1,2},{2,3},{3,4},{4,5},{5,6},{6,7},{8,9},{9,10},{10,11},{11... | collective-permute-start | bytes 786440 | tf_op jit(solution)/shard_map/while/body/eval_jaxpr/ppermute | solution.py:17
  247.0 7.3 %collective-permute-start.1 = (bf16[1024,128]{1,0:T(8,128)(2,1)}, bf16[1024,128]{1,0:T(8,128)(2,1)S(1)}, u32[]{:S(2)}, u32[]{:S(2)}) collective-permute-start(bf16[1024,128]{1,0:T(8,128)(2,1)} %get-tuple-element.904), channel_id=1, source_target_pairs={{0,1},{1,2},{2,3},{3,4},{4,5},{5,6},{6,7},{8,9},{9,10},{10,11},{11... | collective-permute-start | bytes 786440 | tf_op jit(solution)/shard_map/while/body/eval_jaxpr/ppermute | solution.py:17
  250.4 4.6 %copy-start = (f32[1024,128]{1,0:T(8,128)S(1)}, f32[1024,128]{1,0:T(8,128)}, u32[]{:S(2)}) copy-start(f32[1024,128]{1,0:T(8,128)} %get-tuple-element.907) | copy-start | bytes 1572868 | tf_op jit(solution)/shard_map/while
  256.1 0.8 copy-start.1
  256.9 8.0 %collective-permute-start = (bf16[1024,128]{1,0:T(8,128)(2,1)}, bf16[1024,128]{1,0:T(8,128)(2,1)S(1)}, u32[]{:S(2)}, u32[]{:S(2)}) collective-permute-start(bf16[1024,128]{1,0:T(8,128)(2,1)} %get-tuple-element.903), channel_id=1, source_target_pairs={{0,1},{1,2},{2,3},{3,4},{4,5},{5,6},{6,7},{8,9},{9,10},{10,11},{11... | collective-permute-start | bytes 786440 | tf_op jit(solution)/shard_map/while/body/eval_jaxpr/ppermute | solution.py:17
  261.1 7.3 %collective-permute-start.1 = (bf16[1024,128]{1,0:T(8,128)(2,1)}, bf16[1024,128]{1,0:T(8,128)(2,1)S(1)}, u32[]{:S(2)}, u32[]{:S(2)}) collective-permute-start(bf16[1024,128]{1,0:T(8,128)(2,1)} %get-tuple-element.904), channel_id=1, source_target_pairs={{0,1},{1,2},{2,3},{3,4},{4,5},{5,6},{6,7},{8,9},{9,10},{10,11},{11... | collective-permute-start | bytes 786440 | tf_op jit(solution)/shard_map/while/body/eval_jaxpr/ppermute | solution.py:17
  264.5 4.7 %copy-start = (f32[1024,128]{1,0:T(8,128)S(1)}, f32[1024,128]{1,0:T(8,128)}, u32[]{:S(2)}) copy-start(f32[1024,128]{1,0:T(8,128)} %get-tuple-element.907) | copy-start | bytes 1572868 | tf_op jit(solution)/shard_map/while
  270.3 0.8 copy-start.1
  271.1 8.8 %collective-permute-start = (bf16[1024,128]{1,0:T(8,128)(2,1)}, bf16[1024,128]{1,0:T(8,128)(2,1)S(1)}, u32[]{:S(2)}, u32[]{:S(2)}) collective-permute-start(bf16[1024,128]{1,0:T(8,128)(2,1)} %get-tuple-element.903), channel_id=1, source_target_pairs={{0,1},{1,2},{2,3},{3,4},{4,5},{5,6},{6,7},{8,9},{9,10},{10,11},{11... | collective-permute-start | bytes 786440 | tf_op jit(solution)/shard_map/while/body/eval_jaxpr/ppermute | solution.py:17
  275.3 8.2 %collective-permute-start.1 = (bf16[1024,128]{1,0:T(8,128)(2,1)}, bf16[1024,128]{1,0:T(8,128)(2,1)S(1)}, u32[]{:S(2)}, u32[]{:S(2)}) collective-permute-start(bf16[1024,128]{1,0:T(8,128)(2,1)} %get-tuple-element.904), channel_id=1, source_target_pairs={{0,1},{1,2},{2,3},{3,4},{4,5},{5,6},{6,7},{8,9},{9,10},{10,11},{11... | collective-permute-start | bytes 786440 | tf_op jit(solution)/shard_map/while/body/eval_jaxpr/ppermute | solution.py:17
  278.7 5.6 %copy-start = (f32[1024,128]{1,0:T(8,128)S(1)}, f32[1024,128]{1,0:T(8,128)}, u32[]{:S(2)}) copy-start(f32[1024,128]{1,0:T(8,128)} %get-tuple-element.907) | copy-start | bytes 1572868 | tf_op jit(solution)/shard_map/while
  285.4 0.8 copy-start.1
  286.2 8.8 %collective-permute-start = (bf16[1024,128]{1,0:T(8,128)(2,1)}, bf16[1024,128]{1,0:T(8,128)(2,1)S(1)}, u32[]{:S(2)}, u32[]{:S(2)}) collective-permute-start(bf16[1024,128]{1,0:T(8,128)(2,1)} %get-tuple-element.903), channel_id=1, source_target_pairs={{0,1},{1,2},{2,3},{3,4},{4,5},{5,6},{6,7},{8,9},{9,10},{10,11},{11... | collective-permute-start | bytes 786440 | tf_op jit(solution)/shard_map/while/body/eval_jaxpr/ppermute | solution.py:17
  289.5 9.1 %collective-permute-start.1 = (bf16[1024,128]{1,0:T(8,128)(2,1)}, bf16[1024,128]{1,0:T(8,128)(2,1)S(1)}, u32[]{:S(2)}, u32[]{:S(2)}) collective-permute-start(bf16[1024,128]{1,0:T(8,128)(2,1)} %get-tuple-element.904), channel_id=1, source_target_pairs={{0,1},{1,2},{2,3},{3,4},{4,5},{5,6},{6,7},{8,9},{9,10},{10,11},{11... | collective-permute-start | bytes 786440 | tf_op jit(solution)/shard_map/while/body/eval_jaxpr/ppermute | solution.py:17
  292.9 6.5 %copy-start = (f32[1024,128]{1,0:T(8,128)S(1)}, f32[1024,128]{1,0:T(8,128)}, u32[]{:S(2)}) copy-start(f32[1024,128]{1,0:T(8,128)} %get-tuple-element.907) | copy-start | bytes 1572868 | tf_op jit(solution)/shard_map/while
  300.5 0.8 copy-start.1
  301.3 8.8 %collective-permute-start = (bf16[1024,128]{1,0:T(8,128)(2,1)}, bf16[1024,128]{1,0:T(8,128)(2,1)S(1)}, u32[]{:S(2)}, u32[]{:S(2)}) collective-permute-start(bf16[1024,128]{1,0:T(8,128)(2,1)} %get-tuple-element.903), channel_id=1, source_target_pairs={{0,1},{1,2},{2,3},{3,4},{4,5},{5,6},{6,7},{8,9},{9,10},{10,11},{11... | collective-permute-start | bytes 786440 | tf_op jit(solution)/shard_map/while/body/eval_jaxpr/ppermute | solution.py:17
  303.7 10.0 %collective-permute-start.1 = (bf16[1024,128]{1,0:T(8,128)(2,1)}, bf16[1024,128]{1,0:T(8,128)(2,1)S(1)}, u32[]{:S(2)}, u32[]{:S(2)}) collective-permute-start(bf16[1024,128]{1,0:T(8,128)(2,1)} %get-tuple-element.904), channel_id=1, source_target_pairs={{0,1},{1,2},{2,3},{3,4},{4,5},{5,6},{6,7},{8,9},{9,10},{10,11},{11... | collective-permute-start | bytes 786440 | tf_op jit(solution)/shard_map/while/body/eval_jaxpr/ppermute | solution.py:17
  307.0 7.4 %copy-start = (f32[1024,128]{1,0:T(8,128)S(1)}, f32[1024,128]{1,0:T(8,128)}, u32[]{:S(2)}) copy-start(f32[1024,128]{1,0:T(8,128)} %get-tuple-element.907) | copy-start | bytes 1572868 | tf_op jit(solution)/shard_map/while
  315.5 0.8 copy-start.1
Sparse Core Ops, SparseCore 0:
  318.5 32.0 all-gather.3
where the time goes:
time: 369 us; the launch traced here: 364 us
  other arithmetic  97.2 us (26%)
  matrix products  95 us (26%)
  local copies, waits for them, and re-layouts  51.3 us (14%)
  starting transfers between devices  43.4 us (12%)
  waiting for transfers between devices  38.5 us (10%)
  between operations  14.3 us (4%)
  blocking collectives  12.1 us (3%)
  loops' own time  12 us (3%)
    another operation x1, other arithmetic, block_parts(): jax.scipy.linalg.solve_triangular(lower_part, identity, lower=True)  79.4 us
    dot_general x65, matrix products, matmul(): return jnp.matmul(first_matrix, second_matrix, precision=PRECISE)  77.6 us
    ppermute x14, starting transfers between devices, from_behind(): return lax.ppermute(block, axis, route)  38.6 us
    all_gather x1, waiting for transfers between devices, body(): piece = lax.all_gather(attended[:, None, :], 'head', axis=1, tiled=True)  31.3 us
    while x73, local copies, waits for them, and re-layouts  16 us
    all_gather x1, blocking collectives, body(): all_ends = lax.all_gather(transit[None], 'ctx', axis=0, tiled=True)  12.1 us
    dynamic_slice x24, local copies, waits for them, and re-layouts, shard_local(): lax.scan(advance, initial, (numbers, start_query, final_key, inside_mask,...  10.1 us
    dot_general x7, matrix products, absorb(): jnp.dot(weight_matrix.astype(jnp.bfloat16), value_block, preferred_elemen...  7.69 us
  transfers between devices with their start and end apart: 16, of which 7 were waited for; matrix products, arithmetic and copies ran while one was open for 62% of the time, Pallas kernels for 0%

commit v1 on v0

v1 whole, which is shorter than its diff:
```python
import functools

import jax
import jax.numpy as jnp
from jax import lax
from jax.experimental import pallas as pl
from jax.experimental.pallas import tpu as pltpu
from jax.sharding import PartitionSpec as P

EPSILON = 1e-06
NEGATIVE = -1e30
MESH = pl.DeviceIdType.MESH
F32 = jnp.float32
BF16 = jnp.bfloat16


def mm(a, b):
    return jnp.dot(a, b, preferred_element_type=F32)


def split(x):
    high = x.astype(BF16)
    return high, (x - high.astype(F32)).astype(BF16)


def dot3(a, b):
    (ah, al), (bh, bl) = split(a), split(b)
    if a.shape[1] <= 128:
        return mm(jnp.concatenate([ah, al], 1), jnp.concatenate([bh, bh], 0)) + mm(ah, bl)
    return mm(ah, bh) + mm(al, bh) + mm(ah, bl)


def kernel(
    n_ctx, n_head, block,
    q_ref, k_ref, v_ref, h_ref, rates_ref, w_ref,
    att_ref, flat_ref, cols_ref,
    kall, vall, tall, ksend, tsend, nmat, inv, moved, mov, acc, peak, total,
    v_ssem, v_rsem, k_ssem, k_rsem, t_ssem, t_rsem, w_ssem, w_rsem, a_ssem, a_rsem, loc_sem,
):
    me = lax.axis_index("ctx")
    head = lax.axis_index("head")
    rows, feat = q_ref.shape
    blocks = rows // block
    width = cols_ref.shape[1]
    scale = feat ** (-0.5)

    barrier = pltpu.get_barrier_semaphore()
    for step in range(1, n_ctx):
        pl.semaphore_signal(barrier, inc=1, device_id={"ctx": lax.rem(me + step, n_ctx)}, device_id_type=MESH)
    for step in range(1, n_head):
        pl.semaphore_signal(barrier, inc=1, device_id={"head": lax.rem(head + step, n_head)}, device_id_type=MESH)
    pl.semaphore_wait(barrier, n_ctx + n_head - 2)

    def v_copy(owner, peer):
        return pltpu.make_async_remote_copy(
            src_ref=v_ref, dst_ref=vall.at[owner], send_sem=v_ssem.at[peer], recv_sem=v_rsem.at[owner],
            device_id={"ctx": peer}, device_id_type=MESH)

    def k_copy(owner, peer):
        return pltpu.make_async_remote_copy(
            src_ref=ksend, dst_ref=kall.at[owner], send_sem=k_ssem.at[peer], recv_sem=k_rsem.at[owner],
            device_id={"ctx": peer}, device_id_type=MESH)

    def t_copy(owner, peer):
        return pltpu.make_async_remote_copy(
            src_ref=tsend, dst_ref=tall.at[owner], send_sem=t_ssem.at[peer], recv_sem=t_rsem.at[owner],
            device_id={"ctx": peer}, device_id_type=MESH)

    def w_copy(owner, peer):
        return pltpu.make_async_remote_copy(
            src_ref=w_ref.at[:, pl.ds(pl.multiple_of(peer * width, 128), width)],
            dst_ref=cols_ref.at[pl.ds(pl.multiple_of(owner * feat, 128), feat), :],
            send_sem=w_ssem.at[peer], recv_sem=w_rsem.at[owner],
            device_id={"head": peer}, device_id_type=MESH)

    def a_copy(owner, peer):
        return pltpu.make_async_remote_copy(
            src_ref=att_ref, dst_ref=flat_ref.at[:, pl.ds(pl.multiple_of(owner * feat, 128), feat)],
            send_sem=a_ssem.at[peer], recv_sem=a_rsem.at[owner],
            device_id={"head": peer}, device_id_type=MESH)

    def later(action):
        def go(peer, carry):
            action(peer)
            return carry
        lax.fori_loop(me + 1, n_ctx, go, 0)

    later(lambda peer: v_copy(me, peer).start())
    for step in range(1, n_head):
        w_copy(head, lax.rem(head + step, n_head)).start()
    w_own = pltpu.make_async_copy(
        w_ref.at[:, pl.ds(pl.multiple_of(head * width, 128), width)],
        cols_ref.at[pl.ds(pl.multiple_of(head * feat, 128), feat), :], loc_sem.at[0])
    w_own.start()

    ri = lax.broadcasted_iota(jnp.int32, (block, block), 0)
    ci = lax.broadcasted_iota(jnp.int32, (block, block), 1)
    eye = ri == ci
    strict = ri > ci
    nt = (((1,), (1,)), ((), ()))

    scales = []
    for b in range(blocks):
        part = slice(b * block, (b + 1) * block)
        hb = h_ref[part, :]
        gram = lax.dot_general(hb, hb, nt, preferred_element_type=F32)
        diag = jnp.where(eye, gram, 0.0)
        r_col = lax.rsqrt(jnp.sum(diag, axis=1, keepdims=True) + EPSILON)
        r_row = lax.rsqrt(jnp.sum(diag, axis=0, keepdims=True) + EPSILON)
        beta_row = rates_ref[:, part]
        beta_col = jnp.sum(jnp.where(eye, beta_row, 0.0), axis=1, keepdims=True)
        lower = jnp.where(strict, gram * (beta_col * r_col) * r_row, 0.0)
        nmat[b] = lower
        first = jnp.logical_and((ri >> 1) == (ci >> 1), strict)
        inv[b] = jnp.where(eye, 1.0, 0.0) - jnp.where(first, lower, 0.0)
        scales.append((r_col, r_row * beta_row))

    def level(depth, carry):
        near = jnp.logical_and((ri >> (depth + 1)) == (ci >> (depth + 1)), (ri >> depth) != (ci >> depth))
        xs = [inv[b] for b in range(blocks)]
        parts = [split(x) for x in xs]
        ys = []
        for b in range(blocks):
            (mh, ml), (xh, xl) = split(jnp.where(near, nmat[b], 0.0)), parts[b]
            ys.append(mm(mh, xh) + mm(ml, xh) + mm(mh, xl))
        for b in range(blocks):
            (yh, yl), (xh, xl) = split(ys[b]), parts[b]
            inv[b] = xs[b] - (mm(xh, yh) + mm(xl, yh) + mm(xh, yl))
        return carry

    lax.fori_loop(1, block.bit_length() - 1, level, 0)

    fr = lax.broadcasted_iota(jnp.int32, (feat, feat), 0)
    fc = lax.broadcasted_iota(jnp.int32, (feat, feat), 1)
    unit = jnp.where(fr == fc, 1.0, 0.0).astype(F32)
    rights, passages, finals = [], [], []
    for b in range(blocks):
        part = slice(b * block, (b + 1) * block)
        hb, kb = h_ref[part, :], k_ref[part, :]
        r_col, rb_row = scales[b]
        th, tl = split(inv[b] * r_col * rb_row)
        wk = lax.dot_general(hb, kb, nt, preferred_element_type=F32)
        wh, wl = split(jnp.where(strict, wk, 0.0))
        rk = mm(th, wh) + mm(tl, wh) + mm(th, wl)
        rh = mm(th, hb) + mm(tl, hb)
        hbt = hb.astype(F32).T.astype(BF16)
        rkh, rkl = split(rk)
        rhh, rhl = split(rh)
        finals.append(kb.astype(F32).T - (mm(hbt, rkh) + mm(hbt, rkl)))
        passages.append(unit - (mm(hbt, rhh) + mm(hbt, rhl)))
        rights.append((rkh, rkl, rhh, rhl))

    prefixes = [None]
    now = finals[0]
    prefix = passages[0]
    for b in range(1, blocks):
        moved[b - 1, :, : b * block] = now
        prefixes.append(prefix)
        now = jnp.concatenate([dot3(passages[b], now), finals[b]], 1)
        prefix = dot3(passages[b], prefix)
    ksend[...] = now.astype(BF16)
    tsend[...] = prefix
    def both(peer):
        t_copy(me, peer).start()
        k_copy(me, peer).start()
    later(both)

    for b in range(blocks):
        part = slice(b * block, (b + 1) * block)
        hb, kb, qb = h_ref[part, :], k_ref[part, :], q_ref[part, :]
        rkh, rkl, rhh, rhl = rights[b]
        qw = lax.dot_general(qb, hb, nt, preferred_element_type=F32)
        qwh, qwl = split(jnp.where(ri >= ci, qw, 0.0))
        qk = lax.dot_general(qb, kb, nt, preferred_element_type=F32)
        inside = (qk - (mm(qwh, rkh) + mm(qwl, rkh) + mm(qwh, rkl))) * scale
        scores = jnp.where(ri >= ci, inside, NEGATIVE)
        start = (qb.astype(F32) - (mm(qwh, rhh) + mm(qwl, rhh) + mm(qwh, rhl))) * scale
        if b:
            scores = jnp.concatenate([dot3(start, moved[b - 1, :, : b * block]), scores], 1)
            mov[part, :] = dot3(start, prefixes[b])
        else:
            mov[part, :] = start
        top = jnp.max(scores, axis=1, keepdims=True)
        weight = jnp.exp(scores - top)
        peak[part, :] = top
        total[part, :] = jnp.sum(weight, axis=1, keepdims=True)
        acc[part, :] = mm(weight.astype(BF16), v_ref[: (b + 1) * block, :])

    def visit(offset, carry):
        source = me - 1 - offset
        t_copy(source, me).wait_recv()
        k_copy(source, me).wait_recv()
        v_copy(source, me).wait_recv()
        keys = kall[source]
        keys2 = jnp.concatenate([keys, keys], 0)
        vals = vall[source]
        th, tl = split(tall[source])
        th2 = jnp.concatenate([th, th], 0)

        def tile(t, inner):
            part = pl.ds(pl.multiple_of(t * block, block), block)
            qh, ql = split(mov[part, :])
            both = jnp.concatenate([qh, ql], 1)
            scores = mm(both, keys2)
            old = peak[part, :]
            top = jnp.maximum(old, jnp.max(scores, axis=1, keepdims=True))
            weight = jnp.exp(scores - top)
            shrink = jnp.exp(old - top)
            peak[part, :] = top
            total[part, :] = total[part, :] * shrink + jnp.sum(weight, axis=1, keepdims=True)
            acc[part, :] = acc[part, :] * shrink + mm(weight.astype(BF16), vals)
            mov[part, :] = mm(both, th2) + mm(qh, tl)
            return inner

        lax.fori_loop(0, blocks, tile, 0)
        return carry

    lax.fori_loop(0, me, visit, 0)

    att_ref[...] = (acc[...] / total[...]).astype(BF16)
    for step in range(1, n_head):
        a_copy(head, lax.rem(head + step, n_head)).start()
    a_own = pltpu.make_async_copy(
        att_ref, flat_ref.at[:, pl.ds(pl.multiple_of(head * feat, 128), feat)], loc_sem.at[1])
    a_own.start()
    w_own.wait()
    def sent(peer):
        v_copy(me, peer).wait_send()
        t_copy(me, peer).wait_send()
        k_copy(me, peer).wait_send()
    later(sent)
    for step in range(1, n_head):
        other = lax.rem(head + step, n_head)
        w_copy(head, other).wait_send()
        w_copy(other, head).wait_recv()
        a_copy(head, other).wait_send()
        a_copy(other, head).wait_recv()
    a_own.wait()


def solution(mesh):
    n_ctx, n_head = mesh.shape["ctx"], mesh.shape["head"]

    def body(queries, keys, values, house, rates, out_weight):
        rows, _, feat = queries.shape
        block = min(256, rows)
        blocks = rows // block
        width = out_weight.shape[1] // n_head
        vmem = pl.BlockSpec(memory_space=pltpu.VMEM)
        hbm = pl.BlockSpec(memory_space=pl.ANY)
        dma = pltpu.SemaphoreType.DMA
        attended, flat, columns = pl.pallas_call(
            functools.partial(kernel, n_ctx, n_head, block),
            out_shape=(
                jax.ShapeDtypeStruct((rows, feat), BF16),
                jax.ShapeDtypeStruct((rows, n_head * feat), BF16),
                jax.ShapeDtypeStruct((n_head * feat, width), BF16),
            ),
            in_specs=[vmem] * 5 + [hbm],
            out_specs=(vmem, hbm, hbm),
            scratch_shapes=[
                pltpu.VMEM((n_ctx, feat, rows), BF16),
                pltpu.VMEM((n_ctx, rows, feat), BF16),
                pltpu.VMEM((n_ctx, feat, feat), F32),
                pltpu.VMEM((feat, rows), BF16),
                pltpu.VMEM((feat, feat), F32),
                pltpu.VMEM((blocks, block, block), F32),
                pltpu.VMEM((blocks, block, block), F32),
                pltpu.VMEM((max(blocks - 1, 1), feat, rows), F32),
                pltpu.VMEM((rows, feat), F32),
                pltpu.VMEM((rows, feat), F32),
                pltpu.VMEM((rows, 1), F32),
                pltpu.VMEM((rows, 1), F32),
                dma((n_ctx,)), dma((n_ctx,)), dma((n_ctx,)), dma((n_ctx,)), dma((n_ctx,)), dma((n_ctx,)),
                dma((n_head,)), dma((n_head,)), dma((n_head,)), dma((n_head,)), dma((2,)),
            ],
            compiler_params=pltpu.CompilerParams(
                collective_id=0, has_side_effects=True, vmem_limit_bytes=60 * 1024 * 1024),
            name="path_attention",
        )(queries.reshape(rows, feat), keys.reshape(rows, feat), values.reshape(rows, feat),
          house.reshape(rows, feat), rates, out_weight)
        projected = jnp.dot(flat, columns, preferred_element_type=F32)
        return attended.reshape(rows, 1, feat), projected.astype(BF16)

    in_specs = (
        P("ctx", "head", None),
        P("ctx", "head", None),
        P("ctx", "head", None),
        P("ctx", "head", None),
        P("head", "ctx"),
        P("head", None),
    )
    out_specs = (P("ctx", "head", None), P("ctx", "head"))
    return jax.shard_map(body, mesh=mesh, in_specs=in_specs, out_specs=out_specs, check_vma=False)
```

time: 369 us -> 91 us (0.25); the launches traced: 364 us -> 90.9 us
  other arithmetic: 97.2 us -> 0 us
  matrix products: 95 us -> 6.31 us
  Pallas kernels: 0 us -> 83.2 us
  local copies, waits for them, and re-layouts: 51.3 us -> 0.71 us
  starting transfers between devices: 43.4 us -> 0 us
  waiting for transfers between devices: 38.5 us -> 0 us
  between operations: 14.3 us -> 0.65 us
  blocking collectives: 12.1 us -> 0 us
  loops' own time: 12 us -> 0 us
    dot_general x74 -> x1, matrix products: 94 us -> 6.31 us  [body(): projected = jnp.dot(flat, columns, preferred_element_type=F32)]
    pallas_call x0 -> x1, Pallas kernels: none -> 83.2 us  [body(): pl.pallas_call(functools.partial(kernel, n_ctx, n_head, block), out_shape...]
    another operation x2 -> x0, other arithmetic: 79.4 us -> none  [the longest x1 79.4 us: block_parts(): jax.scipy.linalg.solve_triangular(lower_part, identity, lower=True)]
    ppermute x14 -> x0, starting transfers between devices: 38.6 us -> none  [from_behind(): return lax.ppermute(block, axis, route)]
    all_gather x1 -> x0, waiting for transfers between devices: 31.3 us -> none  [body(): piece = lax.all_gather(attended[:, None, :], 'head', axis=1, tiled=True)]
    while x76 -> x0, local copies, waits for them, and re-layouts: 18.2 us -> none
    dynamic_update_slice x24 -> x0, local copies, waits for them, and re-layouts: 13.6 us -> none  [the longest x8 6.86 us: advance(): lax.dynamic_update_slice(scores, inside_rows, (anchor, number * length))]
    all_gather x1 -> x0, blocking collectives: 12.1 us -> none  [body(): all_ends = lax.all_gather(transit[None], 'ctx', axis=0, tiled=True)]
  transfers between devices with their start and end apart: 16 -> 0, of which waited for: 7 -> 0; matrix products, arithmetic and copies ran while one was open for 62% -> 0% of each run, Pallas kernels for 0% -> 0%
where the time goes in v1:
time: 91 us; the launch traced here: 90.9 us
  Pallas kernels  83.2 us (91%)
  matrix products  6.31 us (7%)
    pallas_call x1, Pallas kernels, body(): pl.pallas_call(functools.partial(kernel, n_ctx, n_head, block), out_shape...  83.2 us
    dot_general x1, matrix products, body(): projected = jnp.dot(flat, columns, preferred_element_type=F32)  6.31 us

profile of v1, /device:TPU:13, one launch (start us, length us, event | category | flops | bytes accessed | tf_op | source)
XLA Modules:
  0.0 90.9 jit_solution(7129240809279476410)
XLA Ops:
  0.6 83.2 %path_attention.1 = (bf16[1024,128]{1,0:T(8,128)(2,1)}, bf16[1024,512]{1,0:T(8,128)(2,1)}, bf16[512,2048]{1,0:T(8,128)(2,1)}) custom-call(bf16[1024,128]{1,0:T(8,128)(2,1)} %bitcast.7, bf16[1024,128]{1,0:T(8,128)(2,1)} %bitcast.8, bf16[1024,128]{1,0:T(8,128)(2,1)} %bitcast.9, bf16[1024,128]{1,0:T(8,128)(2,1)} %bitcast.10, f32[1,1024]{1,0:T(1,128)} %rates_ref.1, ...), custom_call_target="tpu_custom_call" | custom-call | tf_op jit(solution)/shard_map/path_attention/pallas_call | solution.py:252
  83.8 0.0 copy-start
  83.8 6.3 %convolution_convert_fusion = bf16[1024,2048]{1,0:T(8,128)(2,1)} fusion(bf16[1024,512]{1,0:T(8,128)(2,1)} %get-tuple-element.6, bf16[512,2048]{1,0:T(8,128)(2,1)} %get-tuple-element.7), kind=kOutput, calls=%fused_computation | convolution fusion | flops 2149580800 | bytes 7340032 | tf_op jit(solution)/shard_map/dot_general | solution.py:282
  90.1 0.0 copy-done
  90.2 0.7 copy.9
Async XLA Ops:
  83.8 6.3 %copy-start = (bf16[1024,128]{1,0:T(8,128)(2,1)S(1)}, bf16[1024,128]{1,0:T(8,128)(2,1)}, u32[]{:S(2)}) copy-start(bf16[1024,128]{1,0:T(8,128)(2,1)} %get-tuple-element.5) | copy-start | bytes 786436
